TPU v7x, 32 devices: a whole 2x2x4 slice. The times are simulated.
32 devices in a mesh: groups: 2 (over x), seq: 16 (over z, y, core).
Axes of the slice: x: 2, y: 2, z: 4, core: 2. Of those that a mesh axis runs over, the one named last changes fastest.
Arguments:
- prefill_keys: bfloat16 [128, 4096, 128], P(('groups', 'seq')), parts along dimension 0, may hold values from -4 to 4
- prefill_values: bfloat16 [128, 4096, 128], P(('groups', 'seq')), parts along dimension 0, may hold values from -6 to 6
- window_queries: bfloat16 [128, 8, 256, 128], P(('groups', 'seq')), parts along dimension 0, may hold values from -48 to 48
- step_queries: bfloat16 [128, 2, 8, 128], P('groups'), parts along dimension 0, may hold values from -48 to 48
- new_keys: bfloat16 [128, 2, 128], P('groups'), parts along dimension 0, may hold values from -24 to 24
- new_values: bfloat16 [128, 2, 128], P('groups'), parts along dimension 0, may hold values from -6 to 6
- lengths: int32 [16], P('groups'), parts along dimension 0, may hold values from 2048 to 4096
- keep_mask: int32 [16, 32], P('groups'), parts along dimension 0, may hold values from 0 to 1, as said below
Outputs:
- cache_keys: bfloat16 [128, 4096, 128], P('groups', 'seq'), parts along dimension 0
- cache_values: bfloat16 [128, 4096, 128], P('groups', 'seq'), parts along dimension 0
- attended: bfloat16 [128, 2, 8, 128], P('groups'), parts along dimension 0
- block_scores: float32 [128, 32], P('groups', 'seq'), parts along dimension 0
There are 2 independent parts, one for each index of `groups`. A program takes and returns all parts, laid end to end along the dimension named above; each array names one. Nothing has to cross between parts.
Inputs may be any that keep to these rules, and one draw needn't show every extreme that they name: `keep_mask`: 1 keeps a block, 0 drops it; block 0 of every sequence is kept.
All inputs are finite; a program needn't handle non-finite values.
Results may differ from a plain program's by a relative error of at most 0.0055.
Values may be sent and summed in bfloat16 or wider, within the bound.
No kernel may reach another device: no remote copies, remote signals or barrier semaphores. Data moves between devices by JAX's collectives and lax.ppermute only.
A program may use at most 128 MiB of HBM per device.

v0:
```python
import math
import jax
import jax.numpy as jnp
from jax import lax
from jax.sharding import PartitionSpec as P

KVH = 8
GROUP = 8
BLOCK = 128


def window_mass(prefill_keys, window_queries, lengths, keep_mask, first_pair):
    pair_count, token_count, head_width = prefill_keys.shape
    block_count = keep_mask.shape[1]
    window_size = window_queries.shape[2]
    rows_pair = window_queries.shape[1] * window_size
    rows_block = math.gcd(rows_pair, 512)
    per_pair = rows_pair // rows_block
    flat_rows = window_queries.reshape(pair_count * per_pair, rows_block, head_width)
    scaling = 1.0 / math.sqrt(head_width)
    position = jnp.arange(token_count, dtype=jnp.int32)

    def one_block(block_index):
        pair_local = block_index // per_pair
        seq_id = (first_pair + pair_local) // KVH
        scores = (
            lax.dot_general(
                flat_rows[block_index],
                prefill_keys[pair_local],
                (((1,), (1,)), ((), ())),
                preferred_element_type=jnp.float32,
            )
            * scaling
        )
        row_offset = block_index % per_pair * rows_block + jnp.arange(rows_block, dtype=jnp.int32)
        query_pos = lengths[seq_id] - window_size + row_offset % window_size
        kept_tokens = jnp.broadcast_to(
            keep_mask[seq_id][:, None] > 0, (block_count, BLOCK)
        ).reshape(token_count)
        visible = kept_tokens[None, :] & (position[None, :] <= query_pos[:, None])
        scores = jnp.where(visible, scores, -jnp.inf)
        highest = jnp.max(scores, axis=1, keepdims=True)
        weights = jnp.exp(scores - highest)
        probability = weights / jnp.sum(weights, axis=1, keepdims=True)
        return jnp.sum(probability, axis=0).reshape(block_count, BLOCK).sum(axis=1)

    block_parts = lax.map(one_block, jnp.arange(pair_count * per_pair, dtype=jnp.int32))
    return block_parts.reshape(pair_count, per_pair, block_count).sum(axis=1) / GROUP


def select_rows(small_table, seq_ids):
    matches = seq_ids[:, None] == jnp.arange(small_table.shape[0], dtype=jnp.int32)[None, :]
    return jnp.sum(jnp.where(matches[:, :, None], small_table[None, :, :], 0), axis=1)


def step_scores(cache_part, queries_here, new_here, lengths, keep_mask, first_pair):
    pair_count, token_count, head_width = cache_part.shape
    step_count = queries_here.shape[1]
    group_size = queries_here.shape[2]
    query_rows = queries_here.reshape(pair_count, step_count * group_size, head_width)
    scaling = 1.0 / math.sqrt(head_width)
    scores = (
        jnp.einsum("pqd,ptd->pqt", query_rows, cache_part, preferred_element_type=jnp.float32)
        * scaling
    )
    seq_ids = (first_pair + jnp.arange(pair_count, dtype=jnp.int32)) // KVH
    block_count = token_count // BLOCK
    kept_blocks = select_rows(keep_mask, seq_ids) > 0
    kept_tokens = jnp.broadcast_to(
        kept_blocks[:, :, None], (pair_count, block_count, BLOCK)
    ).reshape(pair_count, token_count)
    seq_length = select_rows(lengths[:, None], seq_ids)[:, 0]
    position = jnp.arange(token_count, dtype=jnp.int32)
    visible = kept_tokens & (position[None, :] < seq_length[:, None])
    scores = jnp.where(visible[:, None, :], scores, -jnp.inf)
    own_scores = (
        jnp.einsum("pqd,pjd->pqj", query_rows, new_here, preferred_element_type=jnp.float32)
        * scaling
    )
    row_step = jnp.arange(step_count * group_size, dtype=jnp.int32) // group_size
    own_visible = jnp.arange(step_count, dtype=jnp.int32)[None, :] <= row_step[:, None]
    own_scores = jnp.where(own_visible[None], own_scores, -jnp.inf)
    return (scores, own_scores)


def local_terms(scores, cache_vals, highest):
    weights = jnp.exp(scores - highest[:, :, None])
    total_mass = jnp.sum(weights, axis=2)
    summed = jnp.einsum(
        "pqt,ptd->pqd", weights.astype(jnp.bfloat16), cache_vals, preferred_element_type=jnp.float32
    )
    return (weights, total_mass, summed)


def finish(summed, total_mass, weights, highest, own_scores, new_vals):
    own_weights = jnp.exp(own_scores - highest[:, :, None])
    total_mass = total_mass + jnp.sum(own_weights, axis=2)
    summed = summed + jnp.einsum(
        "pqj,pjd->pqd",
        own_weights.astype(jnp.bfloat16),
        new_vals,
        preferred_element_type=jnp.float32,
    )
    pair_count, row_count, head_width = summed.shape
    attended = (
        (summed / total_mass[:, :, None])
        .astype(jnp.bfloat16)
        .reshape(pair_count, row_count // GROUP, GROUP, head_width)
    )
    token_count = weights.shape[2]
    new_mass = (
        jnp.sum(weights / total_mass[:, :, None], axis=1)
        .reshape(pair_count, token_count // BLOCK, BLOCK)
        .sum(axis=2)
        / GROUP
    )
    return (attended, new_mass)


def local(
    prefill_keys,
    prefill_values,
    window_queries,
    step_queries,
    new_keys,
    new_values,
    lengths,
    keep_mask,
):
    pair_count = prefill_keys.shape[0]
    first_pair = lax.axis_index("seq") * pair_count
    prior_mass = window_mass(prefill_keys, window_queries, lengths, keep_mask, first_pair).astype(
        jnp.bfloat16
    )
    cache_keys, cache_values, prior_tokens = (
        lax.all_to_all(prefill_keys, "seq", split_axis=1, concat_axis=0, tiled=True),
        lax.all_to_all(prefill_values, "seq", split_axis=1, concat_axis=0, tiled=True),
        lax.all_to_all(prior_mass, "seq", split_axis=1, concat_axis=0, tiled=True),
    )
    queries_here = lax.dynamic_slice_in_dim(step_queries, first_pair, pair_count, 0)
    new_keys_here = lax.dynamic_slice_in_dim(new_keys, first_pair, pair_count, 0)
    new_values_here = lax.dynamic_slice_in_dim(new_values, first_pair, pair_count, 0)
    scores, own_scores = step_scores(
        prefill_keys, queries_here, new_keys_here, lengths, keep_mask, first_pair
    )
    highest = jnp.maximum(jnp.max(scores, axis=2), jnp.max(own_scores, axis=2))
    weights, total_mass, summed = local_terms(scores, prefill_values, highest)
    attended_here, mass_here = finish(
        summed, total_mass, weights, highest, own_scores, new_values_here
    )
    attended = lax.all_gather(attended_here, "seq", axis=0, tiled=True)
    new_mass = lax.all_to_all(mass_here, "seq", split_axis=1, concat_axis=0, tiled=True)
    block_scores = prior_tokens.astype(jnp.float32) + new_mass
    return (cache_keys, cache_values, attended, block_scores)


def solution(mesh):
    placed = (
        P(("groups", "seq"), None, None),
        P(("groups", "seq"), None, None),
        P(("groups", "seq"), None, None, None),
        P("groups", None, None, None),
        P("groups", None, None),
        P("groups", None, None),
        P("groups"),
        P("groups", None),
    )
    return jax.shard_map(
        local,
        mesh=mesh,
        in_specs=placed,
        out_specs=(
            P("groups", "seq", None),
            P("groups", "seq", None),
            P("groups", None, None, None),
            P("groups", "seq"),
        ),
        check_vma=False,
    )
```

profile of v0, /device:TPU:11, one launch (start us, length us, event | category | flops | bytes accessed | tf_op | source)
XLA Modules:
  0.0 480.5 jit_solution(5911037382524738119)
XLA Ops:
  0.7 232.3 %while.14 = (s32[]{:T(128)}, f32[16,32]{1,0:T(8,128)S(1)}, s32[16]{0:T(128)S(1)}, s32[]{:T(128)}, s32[8,32]{1,0:T(8,128)}, /*index=5*/s32[8]{0:T(128)}, bf16[16,...) while((s32[]{:T(128)}, f32[16,32]{1,0:T(8,128)S(1)}, ...), condition=%wide.region_11.12_spmd.clone, body=%wide.region_6.11_spmd.clone.sunk | while | flops 557848064 | bytes 26402040 | solution.py:47
  5.2 1.2 dynamic_slice.95
  7.9 4.0 fusion.44
  11.9 1.3 fusion.45
  13.1 1.9 divide_reduce_fusion.3
  22.4 4.0 fusion.44
  26.4 1.3 fusion.45
  27.7 1.9 divide_reduce_fusion.3
  36.9 4.0 fusion.44
  40.9 1.3 fusion.45
  42.2 1.9 divide_reduce_fusion.3
  51.5 4.0 fusion.44
  55.4 1.3 fusion.45
  56.7 1.9 divide_reduce_fusion.3
  63.3 1.2 dynamic_slice.95
  66.0 4.0 fusion.44
  69.9 1.3 fusion.45
  71.2 1.9 divide_reduce_fusion.3
  80.5 4.0 fusion.44
  84.5 1.3 fusion.45
  85.7 1.9 divide_reduce_fusion.3
  95.0 4.0 fusion.44
  99.0 1.3 fusion.45
  100.3 1.9 divide_reduce_fusion.3
  109.5 4.0 fusion.44
  113.5 1.3 fusion.45
  114.8 1.9 divide_reduce_fusion.3
  121.4 1.2 dynamic_slice.95
  124.0 4.0 fusion.44
  128.0 1.3 fusion.45
  129.3 1.9 divide_reduce_fusion.3
  138.6 4.0 fusion.44
  142.5 1.3 fusion.45
  143.8 1.9 divide_reduce_fusion.3
  153.1 4.0 fusion.44
  157.0 1.3 fusion.45
  158.3 1.9 divide_reduce_fusion.3
  167.6 4.0 fusion.44
  171.6 1.3 fusion.45
  172.8 1.9 divide_reduce_fusion.3
  182.1 4.0 fusion.44
  186.1 1.3 fusion.45
  187.4 1.9 divide_reduce_fusion.3
  196.6 4.0 fusion.44
  200.6 1.3 fusion.45
  201.9 1.9 divide_reduce_fusion.3
  211.1 4.0 fusion.44
  215.1 1.3 fusion.45
  216.4 1.9 divide_reduce_fusion.3
  225.7 4.0 fusion.44
  229.6 1.3 fusion.45
  230.9 1.9 divide_reduce_fusion.3
  233.7 6.5 %all-to-all-start.2 = ((bf16[4,16,2]{0,2,1:T(2,128)(2,1)}), bf16[4,16,2]{0,2,1:T(2,128)(2,1)S(1)}, u32[]{:S(2)}, u32[]{:S(2)}) async-start(bf16[4,16,2]{0,2,1:T(2,128)(2,1)} %bitcast.10), calls=%async_computation.2 | async-start | bytes 16384 | tf_op jit(solution)/shard_map/all_to_all | solution.py:138
  242.1 3.5 fusion.36
  247.9 6.0 %all-to-all-start.3 = ((f32[4,16,2]{0,2,1:T(2,128)}), f32[4,16,2]{0,2,1:T(2,128)S(1)}, u32[]{:S(2)}, u32[]{:S(2)}) async-start(f32[4,16,2]{0,2,1:T(2,128)} %bitcast.11), calls=%async_computation.3 | async-start | bytes 32768 | tf_op jit(solution)/shard_map/all_to_all | solution.py:152
  253.9 7.6 %copy.27 = bf16[4,4096,128]{2,0,1:T(4,128)(2,1)} copy(bf16[4,4096,128]{2,1,0:T(8,128)(2,1)} %param.11) | data formatting | bytes 8388608 | tf_op args[1]
  261.5 6.0 %all-to-all-start.1 = ((bf16[4,4096,128]{2,0,1:T(4,128)(2,1)}), bf16[4,4096,128]{2,0,1:T(4,128)(2,1)}, u32[]{:S(2)}, u32[]{:S(2)}) async-start(bf16[4,4096,128]{2,0,1:T(4,128)(2,1)} %copy.27), calls=%async_computation.1 | async-start | bytes 8388608 | tf_op jit(solution)/shard_map/all_to_all | solution.py:137
  267.5 7.6 %copy.25 = bf16[4,4096,128]{2,0,1:T(4,128)(2,1)} copy(bf16[4,4096,128]{2,1,0:T(8,128)(2,1)} %get-tuple-element.321) | data formatting | bytes 8388608 | tf_op args[0]
  275.1 82.7 %all-to-all-done.1 = bf16[4,4096,128]{2,0,1:T(4,128)(2,1)} async-done(((bf16[4,4096,128]{2,0,1:T(4,128)(2,1)}), bf16[4,4096,128]{2,0,1:T(4,128)(2,1)}, u32[]{:S(2)}, u32[]{:S(2)}) %all-to-all-start.1) | async-done | bytes 4194336 | tf_op jit(solution)/shard_map/all_to_all | solution.py:137
  357.7 7.0 %all-to-all-start = ((bf16[4,4096,128]{2,0,1:T(4,128)(2,1)}), bf16[4,4096,128]{2,0,1:T(4,128)(2,1)}, u32[]{:S(2)}, u32[]{:S(2)}) async-start(bf16[4,4096,128]{2,0,1:T(4,128)(2,1)} %copy.25), calls=%async_computation | async-start | bytes 8388608 | tf_op jit(solution)/shard_map/all_to_all | solution.py:136
  364.8 2.9 fusion.18
  368.6 99.9 %all_gather.3 = bf16[64,2,8,128]{3,2,1,0:T(8,128)(2,1)S(1)} all-gather(bf16[4,2,8,128]{3,2,1,0:T(8,128)(2,1)S(1)} %fusion.14), channel_id=1, replica_groups=mesh['groups'=2,'seq'=16] {'seq'}, dimensions={0}, use_global_device_ids=true | all-gather | bytes 278528 | tf_op jit(solution)/shard_map/all_gather | solution.py:151
  469.1 5.3 %copy.28 = bf16[16,4,256,128]{3,2,1,0:T(8,128)(2,1)} copy(bf16[16,4,256,128]{3,1,2,0:T(4,128)(2,1)} %bitcast.4) | data formatting | bytes 8388608 | tf_op jit(solution)/shard_map/all_to_all | solution.py:137
  474.5 5.3 %copy.26 = bf16[16,4,256,128]{3,2,1,0:T(8,128)(2,1)} copy(bf16[16,4,256,128]{3,1,2,0:T(4,128)(2,1)} %bitcast.1) | data formatting | bytes 8388608 | tf_op jit(solution)/shard_map/all_to_all | solution.py:136
  (142 shorter events, 47.6 us)
Async XLA Ops:
  0.6 241.4 %copy-start = (bf16[64,2,8,128]{3,2,1,0:T(8,128)(2,1)S(1)}, bf16[64,2,8,128]{3,2,1,0:T(8,128)(2,1)}, u32[]{:S(2)}) copy-start(bf16[64,2,8,128]{3,2,1,0:T(8,128)(2,1)} %param.13) | copy-start | bytes 786436
  233.7 14.2 %all-to-all-start.2 = ((bf16[4,16,2]{0,2,1:T(2,128)(2,1)}), bf16[4,16,2]{0,2,1:T(2,128)(2,1)S(1)}, u32[]{:S(2)}, u32[]{:S(2)}) async-start(bf16[4,16,2]{0,2,1:T(2,128)(2,1)} %bitcast.10), calls=%async_computation.2 | async-start | bytes 16384 | tf_op jit(solution)/shard_map/all_to_all | solution.py:138
  247.9 13.6 %all-to-all-start.3 = ((f32[4,16,2]{0,2,1:T(2,128)}), f32[4,16,2]{0,2,1:T(2,128)S(1)}, u32[]{:S(2)}, u32[]{:S(2)}) async-start(f32[4,16,2]{0,2,1:T(2,128)} %bitcast.11), calls=%async_computation.3 | async-start | bytes 32768 | tf_op jit(solution)/shard_map/all_to_all | solution.py:152
  261.5 96.2 %all-to-all-start.1 = ((bf16[4,4096,128]{2,0,1:T(4,128)(2,1)}), bf16[4,4096,128]{2,0,1:T(4,128)(2,1)}, u32[]{:S(2)}, u32[]{:S(2)}) async-start(bf16[4,4096,128]{2,0,1:T(4,128)(2,1)} %copy.27), calls=%async_computation.1 | async-start | bytes 8388608 | tf_op jit(solution)/shard_map/all_to_all | solution.py:137
  357.7 116.7 %all-to-all-start = ((bf16[4,4096,128]{2,0,1:T(4,128)(2,1)}), bf16[4,4096,128]{2,0,1:T(4,128)(2,1)}, u32[]{:S(2)}, u32[]{:S(2)}) async-start(bf16[4,4096,128]{2,0,1:T(4,128)(2,1)} %copy.25), calls=%async_computation | async-start | bytes 8388608 | tf_op jit(solution)/shard_map/all_to_all | solution.py:136
where the time goes:
time: 483 us; the launch traced here: 481 us
  blocking collectives  99.9 us (21%)
  waiting for transfers between devices  82.7 us (17%)
  loops' own time  73.9 us (15%)
  matrix products  71.5 us (15%)
  other arithmetic  66.7 us (14%)
  local copies, waits for them, and re-layouts  59.6 us (12%)
  starting transfers between devices  25.5 us (5%)
    all_gather x1, blocking collectives, local(): attended = lax.all_gather(attended_here, 'seq', axis=0, tiled=True)  99.9 us
    all_to_all x1, waiting for transfers between devices, local(): lax.all_to_all(prefill_values, 'seq', split_axis=1, concat_axis=0, tiled=...  82.7 us
    another operation x1, loops' own time, window_mass(): lax.map(one_block, jnp.arange(pair_count * per_pair, dtype=jnp.int32))  73.9 us
    dot_general x16, matrix products, one_block(): lax.dot_general(flat_rows[block_index], prefill_keys[pair_local], (((1,),...  63.4 us
    reduce_sum x32, other arithmetic, one_block(): return jnp.sum(probability, axis=0).reshape(block_count, BLOCK).sum(axis=1)  32.1 us
    reduce_sum x16, other arithmetic, one_block(): probability = weights / jnp.sum(weights, axis=1, keepdims=True)  20.6 us
    dynamic_slice x16, local copies, waits for them, and re-layouts, one_block(): query_pos = lengths[seq_id] - window_size + row_offset % window_size  19.9 us
    unnamed x6, local copies, waits for them, and re-layouts  15.9 us
  transfers between devices with their start and end apart: 4, of which 1 were waited for; matrix products, arithmetic and copies ran while one was open for 7% of the time, Pallas kernels for 0%

commit v1 on v0

--- a/solution.py
+++ b/solution.py
@@ -148,7 +148,12 @@
     attended_here, mass_here = finish(
         summed, total_mass, weights, highest, own_scores, new_values_here
     )
-    attended = lax.all_gather(attended_here, "seq", axis=0, tiled=True)
+    ring = [attended_here]
+    for hop in range(15):
+        ring.append(lax.ppermute(ring[-1], "seq", [(dev, (dev + 1) % 16) for dev in range(16)]))
+    attended = jnp.roll(
+        jnp.concatenate(ring[::-1], axis=0), (lax.axis_index("seq") + 1) * ring[0].shape[0], axis=0
+    )
     new_mass = lax.all_to_all(mass_here, "seq", split_axis=1, concat_axis=0, tiled=True)
     block_scores = prior_tokens.astype(jnp.float32) + new_mass
     return (cache_keys, cache_values, attended, block_scores)

time: 483 us -> 536 us (1.11)
  the two profiles are of different devices: /device:TPU:11 before, /device:TPU:0 now
where the time goes in v1:
time: 536 us; the launch traced here: 533 us
  waiting for transfers between devices  221 us (41%)
  loops' own time  73.9 us (14%)
  matrix products  71.4 us (13%)
  other arithmetic  66.7 us (12%)
  local copies, waits for them, and re-layouts  59.9 us (11%)
  starting transfers between devices  39.6 us (7%)
    ppermute x15, waiting for transfers between devices, local(): lax.ppermute(ring[-1], 'seq', [(dev, (dev + 1) % 16) for dev in range(16)])  151 us
    another operation x1, loops' own time, window_mass(): lax.map(one_block, jnp.arange(pair_count * per_pair, dtype=jnp.int32))  73.9 us
    all_to_all x1, waiting for transfers between devices, local(): lax.all_to_all(prefill_values, 'seq', split_axis=1, concat_axis=0, tiled=...  70 us
    dot_general x16, matrix products, one_block(): lax.dot_general(flat_rows[block_index], prefill_keys[pair_local], (((1,),...  63.3 us
    reduce_sum x32, other arithmetic, one_block(): return jnp.sum(probability, axis=0).reshape(block_count, BLOCK).sum(axis=1)  32.1 us
    reduce_sum x16, other arithmetic, one_block(): probability = weights / jnp.sum(weights, axis=1, keepdims=True)  20.6 us
    dynamic_slice x16, local copies, waits for them, and re-layouts, one_block(): query_pos = lengths[seq_id] - window_size + row_offset % window_size  19.9 us
    all_to_all x1, starting transfers between devices, local(): lax.all_to_all(prefill_keys, 'seq', split_axis=1, concat_axis=0, tiled=True)  19.7 us
  transfers between devices with their start and end apart: 19, of which 16 were waited for; matrix products, arithmetic and copies ran while one was open for 6% of the time, Pallas kernels for 0%

profile of v1, /device:TPU:0, one launch (start us, length us, event | category | flops | bytes accessed | tf_op | source)
XLA Modules:
  0.0 533.1 jit_solution(14871432760783443629)
XLA Ops:
  0.7 232.2 %while.14 = (s32[]{:T(128)}, f32[16,32]{1,0:T(8,128)S(1)}, s32[16]{0:T(128)S(1)}, s32[]{:T(128)}, s32[8,32]{1,0:T(8,128)}, /*index=5*/s32[8]{0:T(128)}, bf16[16,...) while((s32[]{:T(128)}, f32[16,32]{1,0:T(8,128)S(1)}, ...), condition=%wide.region_11.12_spmd.clone, body=%wide.region_6.11_spmd.clone.sunk | while | flops 557848064 | bytes 26402040 | solution.py:47
  7.9 4.0 fusion.44
  11.8 1.3 fusion.45
  13.1 1.9 divide_reduce_fusion.3
  22.4 4.0 fusion.44
  26.4 1.3 fusion.45
  27.6 1.9 divide_reduce_fusion.3
  36.9 4.0 fusion.44
  42.2 1.9 divide_reduce_fusion.3
  51.4 4.0 fusion.44
  56.7 1.9 divide_reduce_fusion.3
  65.9 4.0 fusion.44
  71.2 1.9 divide_reduce_fusion.3
  80.4 4.0 fusion.44
  85.7 1.9 divide_reduce_fusion.3
  94.9 4.0 fusion.44
  100.2 1.9 divide_reduce_fusion.3
  109.5 4.0 fusion.44
  114.7 1.9 divide_reduce_fusion.3
  124.0 4.0 fusion.44
  127.9 1.3 fusion.45
  129.2 1.9 divide_reduce_fusion.3
  138.5 4.0 fusion.44
  143.7 1.9 divide_reduce_fusion.3
  153.0 4.0 fusion.44
  158.2 1.9 divide_reduce_fusion.3
  167.5 4.0 fusion.44
  171.5 1.3 fusion.45
  172.7 1.9 divide_reduce_fusion.3
  182.0 4.0 fusion.44
  187.2 1.9 divide_reduce_fusion.3
  196.5 4.0 fusion.44
  201.8 1.9 divide_reduce_fusion.3
  211.0 4.0 fusion.44
  215.0 1.3 fusion.45
  216.3 1.9 divide_reduce_fusion.3
  225.5 4.0 fusion.44
  230.8 1.9 divide_reduce_fusion.3
  233.6 7.4 %all-to-all-start.2 = ((bf16[4,16,2]{0,2,1:T(2,128)(2,1)}), bf16[4,16,2]{0,2,1:T(2,128)(2,1)S(1)}, u32[]{:S(2)}, u32[]{:S(2)}) async-start(bf16[4,16,2]{0,2,1:T(2,128)(2,1)} %bitcast.10), calls=%async_computation.2 | async-start | bytes 16384 | tf_op jit(solution)/shard_map/all_to_all | solution.py:138
  242.9 3.5 fusion.36
  248.7 6.0 %all-to-all-start.3 = ((f32[4,16,2]{0,2,1:T(2,128)}), f32[4,16,2]{0,2,1:T(2,128)S(1)}, u32[]{:S(2)}, u32[]{:S(2)}) async-start(f32[4,16,2]{0,2,1:T(2,128)} %bitcast.11), calls=%async_computation.3 | async-start | bytes 32768 | tf_op jit(solution)/shard_map/all_to_all | solution.py:157
  254.8 7.6 %copy.27 = bf16[4,4096,128]{2,0,1:T(4,128)(2,1)} copy(bf16[4,4096,128]{2,1,0:T(8,128)(2,1)} %param.11) | data formatting | bytes 8388608 | tf_op args[1]
  262.3 6.1 %all-to-all-start.1 = ((bf16[4,4096,128]{2,0,1:T(4,128)(2,1)}), bf16[4,4096,128]{2,0,1:T(4,128)(2,1)}, u32[]{:S(2)}, u32[]{:S(2)}) async-start(bf16[4,4096,128]{2,0,1:T(4,128)(2,1)} %copy.27), calls=%async_computation.1 | async-start | bytes 8388608 | tf_op jit(solution)/shard_map/all_to_all | solution.py:137
  268.4 7.6 %copy.25 = bf16[4,4096,128]{2,0,1:T(4,128)(2,1)} copy(bf16[4,4096,128]{2,1,0:T(8,128)(2,1)} %get-tuple-element.313) | data formatting | bytes 8388608 | tf_op args[0]
  276.0 70.0 %all-to-all-done.1 = bf16[4,4096,128]{2,0,1:T(4,128)(2,1)} async-done(((bf16[4,4096,128]{2,0,1:T(4,128)(2,1)}), bf16[4,4096,128]{2,0,1:T(4,128)(2,1)}, u32[]{:S(2)}, u32[]{:S(2)}) %all-to-all-start.1) | async-done | bytes 4194336 | tf_op jit(solution)/shard_map/all_to_all | solution.py:137
  345.9 19.7 %all-to-all-start = ((bf16[4,4096,128]{2,0,1:T(4,128)(2,1)}), bf16[4,4096,128]{2,0,1:T(4,128)(2,1)}, u32[]{:S(2)}, u32[]{:S(2)}) async-start(bf16[4,4096,128]{2,0,1:T(4,128)(2,1)} %copy.25), calls=%async_computation | async-start | bytes 8388608 | tf_op jit(solution)/shard_map/all_to_all | solution.py:136
  365.6 2.9 fusion.18
  369.9 69.1 %collective-permute-done = bf16[4,2,8,128]{3,2,1,0:T(8,128)(2,1)S(1)} collective-permute-done((bf16[4,2,8,128]{3,2,1,0:T(8,128)(2,1)S(1)}, bf16[4,2,8,128]{3,2,1,0:T(8,128)(2,1)S(1)}, u32[]{:S(2)}, u32[]{:S(2)}) %collective-permute-start) | collective-permute-done | bytes 16416 | tf_op jit(solution)/shard_map/ppermute | solution.py:153
  438.9 6.0 %collective-permute-done.1 = bf16[4,2,8,128]{3,2,1,0:T(8,128)(2,1)S(1)} collective-permute-done((bf16[4,2,8,128]{3,2,1,0:T(8,128)(2,1)S(1)}, bf16[4,2,8,128]{3,2,1,0:T(8,128)(2,1)S(1)}, u32[]{:S(2)}, u32[]{:S(2)}) %collective-permute-start.1) | collective-permute-done | bytes 16416 | tf_op jit(solution)/shard_map/ppermute | solution.py:153
  444.9 6.0 %collective-permute-done.2 = bf16[4,2,8,128]{3,2,1,0:T(8,128)(2,1)S(1)} collective-permute-done((bf16[4,2,8,128]{3,2,1,0:T(8,128)(2,1)S(1)}, bf16[4,2,8,128]{3,2,1,0:T(8,128)(2,1)S(1)}, u32[]{:S(2)}, u32[]{:S(2)}) %collective-permute-start.2) | collective-permute-done | bytes 16416 | tf_op jit(solution)/shard_map/ppermute | solution.py:153
  450.8 6.0 %collective-permute-done.3 = bf16[4,2,8,128]{3,2,1,0:T(8,128)(2,1)S(1)} collective-permute-done((bf16[4,2,8,128]{3,2,1,0:T(8,128)(2,1)S(1)}, bf16[4,2,8,128]{3,2,1,0:T(8,128)(2,1)S(1)}, u32[]{:S(2)}, u32[]{:S(2)}) %collective-permute-start.3) | collective-permute-done | bytes 16416 | tf_op jit(solution)/shard_map/ppermute | solution.py:153
  456.8 5.9 %collective-permute-done.4 = bf16[4,2,8,128]{3,2,1,0:T(8,128)(2,1)S(1)} collective-permute-done((bf16[4,2,8,128]{3,2,1,0:T(8,128)(2,1)S(1)}, bf16[4,2,8,128]{3,2,1,0:T(8,128)(2,1)S(1)}, u32[]{:S(2)}, u32[]{:S(2)}) %collective-permute-start.4) | collective-permute-done | bytes 16416 | tf_op jit(solution)/shard_map/ppermute | solution.py:153
  462.7 5.9 %collective-permute-done.5 = bf16[4,2,8,128]{3,2,1,0:T(8,128)(2,1)S(1)} collective-permute-done((bf16[4,2,8,128]{3,2,1,0:T(8,128)(2,1)S(1)}, bf16[4,2,8,128]{3,2,1,0:T(8,128)(2,1)S(1)}, u32[]{:S(2)}, u32[]{:S(2)}) %collective-permute-start.5) | collective-permute-done | bytes 16416 | tf_op jit(solution)/shard_map/ppermute | solution.py:153
  468.5 5.9 %collective-permute-done.6 = bf16[4,2,8,128]{3,2,1,0:T(8,128)(2,1)S(1)} collective-permute-done((bf16[4,2,8,128]{3,2,1,0:T(8,128)(2,1)S(1)}, bf16[4,2,8,128]{3,2,1,0:T(8,128)(2,1)S(1)}, u32[]{:S(2)}, u32[]{:S(2)}) %collective-permute-start.6) | collective-permute-done | bytes 16416 | tf_op jit(solution)/shard_map/ppermute | solution.py:153
  474.4 5.9 %collective-permute-done.7 = bf16[4,2,8,128]{3,2,1,0:T(8,128)(2,1)S(1)} collective-permute-done((bf16[4,2,8,128]{3,2,1,0:T(8,128)(2,1)S(1)}, bf16[4,2,8,128]{3,2,1,0:T(8,128)(2,1)S(1)}, u32[]{:S(2)}, u32[]{:S(2)}) %collective-permute-start.7) | collective-permute-done | bytes 16416 | tf_op jit(solution)/shard_map/ppermute | solution.py:153
  480.2 5.9 %collective-permute-done.8 = bf16[4,2,8,128]{3,2,1,0:T(8,128)(2,1)S(1)} collective-permute-done((bf16[4,2,8,128]{3,2,1,0:T(8,128)(2,1)S(1)}, bf16[4,2,8,128]{3,2,1,0:T(8,128)(2,1)S(1)}, u32[]{:S(2)}, u32[]{:S(2)}) %collective-permute-start.8) | collective-permute-done | bytes 16416 | tf_op jit(solution)/shard_map/ppermute | solution.py:153
  486.1 5.9 %collective-permute-done.9 = bf16[4,2,8,128]{3,2,1,0:T(8,128)(2,1)S(1)} collective-permute-done((bf16[4,2,8,128]{3,2,1,0:T(8,128)(2,1)S(1)}, bf16[4,2,8,128]{3,2,1,0:T(8,128)(2,1)S(1)}, u32[]{:S(2)}, u32[]{:S(2)}) %collective-permute-start.9) | collective-permute-done | bytes 16416 | tf_op jit(solution)/shard_map/ppermute | solution.py:153
  492.0 5.9 %collective-permute-done.10 = bf16[4,2,8,128]{3,2,1,0:T(8,128)(2,1)S(1)} collective-permute-done((bf16[4,2,8,128]{3,2,1,0:T(8,128)(2,1)S(1)}, bf16[4,2,8,128]{3,2,1,0:T(8,128)(2,1)S(1)}, u32[]{:S(2)}, u32[]{:S(2)}) %collective-permute-start.10) | collective-permute-done | bytes 16416 | tf_op jit(solution)/shard_map/ppermute | solution.py:153
  497.8 5.9 %collective-permute-done.11 = bf16[4,2,8,128]{3,2,1,0:T(8,128)(2,1)S(1)} collective-permute-done((bf16[4,2,8,128]{3,2,1,0:T(8,128)(2,1)S(1)}, bf16[4,2,8,128]{3,2,1,0:T(8,128)(2,1)S(1)}, u32[]{:S(2)}, u32[]{:S(2)}) %collective-permute-start.11) | collective-permute-done | bytes 16416 | tf_op jit(solution)/shard_map/ppermute | solution.py:153
  503.7 5.9 %collective-permute-done.12 = bf16[4,2,8,128]{3,2,1,0:T(8,128)(2,1)S(1)} collective-permute-done((bf16[4,2,8,128]{3,2,1,0:T(8,128)(2,1)S(1)}, bf16[4,2,8,128]{3,2,1,0:T(8,128)(2,1)S(1)}, u32[]{:S(2)}, u32[]{:S(2)}) %collective-permute-start.12) | collective-permute-done | bytes 16416 | tf_op jit(solution)/shard_map/ppermute | solution.py:153
  509.6 5.9 %collective-permute-done.13 = bf16[4,2,8,128]{3,2,1,0:T(8,128)(2,1)S(1)} collective-permute-done((bf16[4,2,8,128]{3,2,1,0:T(8,128)(2,1)S(1)}, bf16[4,2,8,128]{3,2,1,0:T(8,128)(2,1)S(1)}, u32[]{:S(2)}, u32[]{:S(2)}) %collective-permute-start.13) | collective-permute-done | bytes 16416 | tf_op jit(solution)/shard_map/ppermute | solution.py:153
  516.1 5.2 collective-permute-done.14
  522.4 5.3 %copy.28 = bf16[16,4,256,128]{3,2,1,0:T(8,128)(2,1)} copy(bf16[16,4,256,128]{3,1,2,0:T(4,128)(2,1)} %bitcast.4) | data formatting | bytes 8388608 | tf_op jit(solution)/shard_map/all_to_all | solution.py:137
  527.7 5.3 %copy.26 = bf16[16,4,256,128]{3,2,1,0:T(8,128)(2,1)} copy(bf16[16,4,256,128]{3,1,2,0:T(4,128)(2,1)} %bitcast.1) | data formatting | bytes 8388608 | tf_op jit(solution)/shard_map/all_to_all | solution.py:136
  (203 shorter events, 66.2 us)
Async XLA Ops:
  0.6 242.3 %copy-start = (bf16[64,2,8,128]{3,2,1,0:T(8,128)(2,1)S(1)}, bf16[64,2,8,128]{3,2,1,0:T(8,128)(2,1)}, u32[]{:S(2)}) copy-start(bf16[64,2,8,128]{3,2,1,0:T(8,128)(2,1)} %param.13) | copy-start | bytes 786436
  233.6 15.2 %all-to-all-start.2 = ((bf16[4,16,2]{0,2,1:T(2,128)(2,1)}), bf16[4,16,2]{0,2,1:T(2,128)(2,1)S(1)}, u32[]{:S(2)}, u32[]{:S(2)}) async-start(bf16[4,16,2]{0,2,1:T(2,128)(2,1)} %bitcast.10), calls=%async_computation.2 | async-start | bytes 16384 | tf_op jit(solution)/shard_map/all_to_all | solution.py:138
  248.7 13.6 %all-to-all-start.3 = ((f32[4,16,2]{0,2,1:T(2,128)}), f32[4,16,2]{0,2,1:T(2,128)S(1)}, u32[]{:S(2)}, u32[]{:S(2)}) async-start(f32[4,16,2]{0,2,1:T(2,128)} %bitcast.11), calls=%async_computation.3 | async-start | bytes 32768 | tf_op jit(solution)/shard_map/all_to_all | solution.py:157
  262.3 83.6 %all-to-all-start.1 = ((bf16[4,4096,128]{2,0,1:T(4,128)(2,1)}), bf16[4,4096,128]{2,0,1:T(4,128)(2,1)}, u32[]{:S(2)}, u32[]{:S(2)}) async-start(bf16[4,4096,128]{2,0,1:T(4,128)(2,1)} %copy.27), calls=%async_computation.1 | async-start | bytes 8388608 | tf_op jit(solution)/shard_map/all_to_all | solution.py:137
  345.9 181.8 %all-to-all-start = ((bf16[4,4096,128]{2,0,1:T(4,128)(2,1)}), bf16[4,4096,128]{2,0,1:T(4,128)(2,1)}, u32[]{:S(2)}, u32[]{:S(2)}) async-start(bf16[4,4096,128]{2,0,1:T(4,128)(2,1)} %copy.25), calls=%async_computation | async-start | bytes 8388608 | tf_op jit(solution)/shard_map/all_to_all | solution.py:136
  369.4 69.5 %collective-permute-start = (bf16[4,2,8,128]{3,2,1,0:T(8,128)(2,1)S(1)}, bf16[4,2,8,128]{3,2,1,0:T(8,128)(2,1)S(1)}, u32[]{:S(2)}, u32[]{:S(2)}) collective-permute-start(bf16[4,2,8,128]{3,2,1,0:T(8,128)(2,1)S(1)} %fusion.14), channel_id=1, source_target_pairs={{0,1},{1,2},{2,3},{3,4},{4,5},{5,6},{6,7},{7,8},{8,9},{9,10},{10,1... | collective-permute-start | bytes 49160 | tf_op jit(solution)/shard_map/ppermute | solution.py:153
  438.9 6.0 %collective-permute-start.1 = (bf16[4,2,8,128]{3,2,1,0:T(8,128)(2,1)S(1)}, bf16[4,2,8,128]{3,2,1,0:T(8,128)(2,1)S(1)}, u32[]{:S(2)}, u32[]{:S(2)}) collective-permute-start(bf16[4,2,8,128]{3,2,1,0:T(8,128)(2,1)S(1)} %collective-permute-done), channel_id=1, source_target_pairs={{0,1},{1,2},{2,3},{3,4},{4,5},{5,6},{6,7},{7,8},{8,9},{9,10},{10,1... | collective-permute-start | bytes 49160 | tf_op jit(solution)/shard_map/ppermute | solution.py:153
  444.9 6.0 %collective-permute-start.2 = (bf16[4,2,8,128]{3,2,1,0:T(8,128)(2,1)S(1)}, bf16[4,2,8,128]{3,2,1,0:T(8,128)(2,1)S(1)}, u32[]{:S(2)}, u32[]{:S(2)}) collective-permute-start(bf16[4,2,8,128]{3,2,1,0:T(8,128)(2,1)S(1)} %collective-permute-done.1), channel_id=1, source_target_pairs={{0,1},{1,2},{2,3},{3,4},{4,5},{5,6},{6,7},{7,8},{8,9},{9,10},{10,1... | collective-permute-start | bytes 49160 | tf_op jit(solution)/shard_map/ppermute | solution.py:153
  450.8 6.0 %collective-permute-start.3 = (bf16[4,2,8,128]{3,2,1,0:T(8,128)(2,1)S(1)}, bf16[4,2,8,128]{3,2,1,0:T(8,128)(2,1)S(1)}, u32[]{:S(2)}, u32[]{:S(2)}) collective-permute-start(bf16[4,2,8,128]{3,2,1,0:T(8,128)(2,1)S(1)} %collective-permute-done.2), channel_id=1, source_target_pairs={{0,1},{1,2},{2,3},{3,4},{4,5},{5,6},{6,7},{7,8},{8,9},{9,10},{10,1... | collective-permute-start | bytes 49160 | tf_op jit(solution)/shard_map/ppermute | solution.py:153
  456.8 5.9 %collective-permute-start.4 = (bf16[4,2,8,128]{3,2,1,0:T(8,128)(2,1)S(1)}, bf16[4,2,8,128]{3,2,1,0:T(8,128)(2,1)S(1)}, u32[]{:S(2)}, u32[]{:S(2)}) collective-permute-start(bf16[4,2,8,128]{3,2,1,0:T(8,128)(2,1)S(1)} %collective-permute-done.3), channel_id=1, source_target_pairs={{0,1},{1,2},{2,3},{3,4},{4,5},{5,6},{6,7},{7,8},{8,9},{9,10},{10,1... | collective-permute-start | bytes 49160 | tf_op jit(solution)/shard_map/ppermute | solution.py:153
  462.7 5.9 %collective-permute-start.5 = (bf16[4,2,8,128]{3,2,1,0:T(8,128)(2,1)S(1)}, bf16[4,2,8,128]{3,2,1,0:T(8,128)(2,1)S(1)}, u32[]{:S(2)}, u32[]{:S(2)}) collective-permute-start(bf16[4,2,8,128]{3,2,1,0:T(8,128)(2,1)S(1)} %collective-permute-done.4), channel_id=1, source_target_pairs={{0,1},{1,2},{2,3},{3,4},{4,5},{5,6},{6,7},{7,8},{8,9},{9,10},{10,1... | collective-permute-start | bytes 49160 | tf_op jit(solution)/shard_map/ppermute | solution.py:153
  468.5 5.9 %collective-permute-start.6 = (bf16[4,2,8,128]{3,2,1,0:T(8,128)(2,1)S(1)}, bf16[4,2,8,128]{3,2,1,0:T(8,128)(2,1)S(1)}, u32[]{:S(2)}, u32[]{:S(2)}) collective-permute-start(bf16[4,2,8,128]{3,2,1,0:T(8,128)(2,1)S(1)} %collective-permute-done.5), channel_id=1, source_target_pairs={{0,1},{1,2},{2,3},{3,4},{4,5},{5,6},{6,7},{7,8},{8,9},{9,10},{10,1... | collective-permute-start | bytes 49160 | tf_op jit(solution)/shard_map/ppermute | solution.py:153
  474.4 5.9 %collective-permute-start.7 = (bf16[4,2,8,128]{3,2,1,0:T(8,128)(2,1)S(1)}, bf16[4,2,8,128]{3,2,1,0:T(8,128)(2,1)S(1)}, u32[]{:S(2)}, u32[]{:S(2)}) collective-permute-start(bf16[4,2,8,128]{3,2,1,0:T(8,128)(2,1)S(1)} %collective-permute-done.6), channel_id=1, source_target_pairs={{0,1},{1,2},{2,3},{3,4},{4,5},{5,6},{6,7},{7,8},{8,9},{9,10},{10,1... | collective-permute-start | bytes 49160 | tf_op jit(solution)/shard_map/ppermute | solution.py:153
  480.2 5.9 %collective-permute-start.8 = (bf16[4,2,8,128]{3,2,1,0:T(8,128)(2,1)S(1)}, bf16[4,2,8,128]{3,2,1,0:T(8,128)(2,1)S(1)}, u32[]{:S(2)}, u32[]{:S(2)}) collective-permute-start(bf16[4,2,8,128]{3,2,1,0:T(8,128)(2,1)S(1)} %collective-permute-done.7), channel_id=1, source_target_pairs={{0,1},{1,2},{2,3},{3,4},{4,5},{5,6},{6,7},{7,8},{8,9},{9,10},{10,1... | collective-permute-start | bytes 49160 | tf_op jit(solution)/shard_map/ppermute | solution.py:153
  486.1 5.9 %collective-permute-start.9 = (bf16[4,2,8,128]{3,2,1,0:T(8,128)(2,1)S(1)}, bf16[4,2,8,128]{3,2,1,0:T(8,128)(2,1)S(1)}, u32[]{:S(2)}, u32[]{:S(2)}) collective-permute-start(bf16[4,2,8,128]{3,2,1,0:T(8,128)(2,1)S(1)} %collective-permute-done.8), channel_id=1, source_target_pairs={{0,1},{1,2},{2,3},{3,4},{4,5},{5,6},{6,7},{7,8},{8,9},{9,10},{10,1... | collective-permute-start | bytes 49160 | tf_op jit(solution)/shard_map/ppermute | solution.py:153
  492.0 5.9 %collective-permute-start.10 = (bf16[4,2,8,128]{3,2,1,0:T(8,128)(2,1)S(1)}, bf16[4,2,8,128]{3,2,1,0:T(8,128)(2,1)S(1)}, u32[]{:S(2)}, u32[]{:S(2)}) collective-permute-start(bf16[4,2,8,128]{3,2,1,0:T(8,128)(2,1)S(1)} %collective-permute-done.9), channel_id=1, source_target_pairs={{0,1},{1,2},{2,3},{3,4},{4,5},{5,6},{6,7},{7,8},{8,9},{9,10},{10,1... | collective-permute-start | bytes 49160 | tf_op jit(solution)/shard_map/ppermute | solution.py:153
  497.8 5.9 %collective-permute-start.11 = (bf16[4,2,8,128]{3,2,1,0:T(8,128)(2,1)S(1)}, bf16[4,2,8,128]{3,2,1,0:T(8,128)(2,1)S(1)}, u32[]{:S(2)}, u32[]{:S(2)}) collective-permute-start(bf16[4,2,8,128]{3,2,1,0:T(8,128)(2,1)S(1)} %collective-permute-done.10), channel_id=1, source_target_pairs={{0,1},{1,2},{2,3},{3,4},{4,5},{5,6},{6,7},{7,8},{8,9},{9,10},{10,1... | collective-permute-start | bytes 49160 | tf_op jit(solution)/shard_map/ppermute | solution.py:153
  503.7 5.9 %collective-permute-start.12 = (bf16[4,2,8,128]{3,2,1,0:T(8,128)(2,1)S(1)}, bf16[4,2,8,128]{3,2,1,0:T(8,128)(2,1)S(1)}, u32[]{:S(2)}, u32[]{:S(2)}) collective-permute-start(bf16[4,2,8,128]{3,2,1,0:T(8,128)(2,1)S(1)} %collective-permute-done.11), channel_id=1, source_target_pairs={{0,1},{1,2},{2,3},{3,4},{4,5},{5,6},{6,7},{7,8},{8,9},{9,10},{10,1... | collective-permute-start | bytes 49160 | tf_op jit(solution)/shard_map/ppermute | solution.py:153
  509.6 5.9 %collective-permute-start.13 = (bf16[4,2,8,128]{3,2,1,0:T(8,128)(2,1)S(1)}, bf16[4,2,8,128]{3,2,1,0:T(8,128)(2,1)S(1)}, u32[]{:S(2)}, u32[]{:S(2)}) collective-permute-start(bf16[4,2,8,128]{3,2,1,0:T(8,128)(2,1)S(1)} %collective-permute-done.12), channel_id=1, source_target_pairs={{0,1},{1,2},{2,3},{3,4},{4,5},{5,6},{6,7},{7,8},{8,9},{9,10},{10,1... | collective-permute-start | bytes 49160 | tf_op jit(solution)/shard_map/ppermute | solution.py:153
  515.4 5.9 %collective-permute-start.14 = (bf16[4,2,8,128]{3,2,1,0:T(8,128)(2,1)S(1)}, bf16[4,2,8,128]{3,2,1,0:T(8,128)(2,1)S(1)}, u32[]{:S(2)}, u32[]{:S(2)}) collective-permute-start(bf16[4,2,8,128]{3,2,1,0:T(8,128)(2,1)S(1)} %collective-permute-done.13), channel_id=1, source_target_pairs={{0,1},{1,2},{2,3},{3,4},{4,5},{5,6},{6,7},{7,8},{8,9},{9,10},{10,1... | collective-permute-start | bytes 49160 | tf_op jit(solution)/shard_map/ppermute | solution.py:153
